TPU v7x, 32 devices: a whole 2x2x4 slice. The times are simulated.
32 devices in a mesh: seq: 8 (over z, y), feat: 4 (over x, core).
Axes of the slice: x: 2, y: 2, z: 4, core: 2. Of those that a mesh axis runs over, the one named last changes fastest.
Arguments:
- hidden_in: bfloat16 [4, 2048, 2048], P(None, 'seq'), may hold values from -6 to 6
- w_query: bfloat16 [2048, 256], replicated, may hold values from -0.125 to 0.125
- w_key: bfloat16 [2048, 256], replicated, may hold values from -0.125 to 0.125
- w_value: bfloat16 [2048, 2048], P(None, 'feat'), may hold values from -0.125 to 0.125
- lengths: int32 [4], replicated, may hold values from 1024 to 2048, as said below
- owners: int32 [4], replicated, may hold values from 0 to 7
Outputs:
- mixed: bfloat16 [4, 2048, 2048], P(None, 'seq', 'feat')
- state_quad: float32 [8, 4, 16, 256, 128], P('seq', None, None, 'feat')
- state_low: float32 [8, 4, 16, 17, 128], P('seq', None, 'feat')
- norm_quad: float32 [8, 4, 16, 256], P('seq', None, None, 'feat')
- norm_low: float32 [8, 4, 16, 17], P('seq', None, 'feat')
Inputs may be any that keep to these rules, and one draw needn't show every extreme that they name: `lengths`: every prompt holds 1024 to 2048 live tokens, and some prompt holds exactly 2048. `owners`: several prompts may share a decoding device.
All inputs are finite; a program needn't handle non-finite values.
Results may differ from a plain program's by a relative error of at most 0.0085.
Values may be sent and summed in bfloat16 or wider, within the bound.
A program may use at most 256 MiB of HBM per device.

v0:
```python
import jax
import jax.numpy as jnp
from jax import lax
from jax.sharding import PartitionSpec as P

H = 16
FD = 16
NORM_FLOOR = 0.0001


def prefix(part, axis, combine, identity):
    place = lax.axis_index(axis)
    gathered = jax.tree.map(lambda a: lax.all_gather(a, axis), part)
    state = jax.tree.map(lambda a, e: jnp.zeros_like(a) + jnp.asarray(e, a.dtype), part, identity)

    def one(step, state):
        return combine(
            state, jax.tree.map(lambda a: lax.dynamic_index_in_dim(a, step, 0, False), gathered)
        )

    return lax.fori_loop(0, place, one, state)


def low_features(inputs):
    constant = jnp.ones(inputs.shape[:-1] + (1,), jnp.float32)
    return jnp.concatenate([constant, inputs * FD ** (-0.25)], axis=-1)


def quad_features(leading, inputs):
    products = leading[..., :, None] * inputs[..., None, :]
    return products.reshape(inputs.shape[:-1] + (leading.shape[-1] * inputs.shape[-1],)) * (
        2.0 * FD
    ) ** (-0.5)


def add_states(earlier_part, later_part):
    return jax.tree.map(
        lambda first_term, second_term: first_term + second_term, earlier_part, later_part
    )


def project(flat_rows, weight_cols, prompts, span, heads, width_last):
    projected = jnp.dot(flat_rows, weight_cols, preferred_element_type=jnp.float32).astype(
        jnp.bfloat16
    )
    return projected.reshape(prompts, span, heads, width_last).astype(jnp.float32)


def body(hidden_in, w_query, w_key, w_value, lengths, owners):
    highest = lax.Precision.HIGHEST
    prompts, span, width = hidden_in.shape
    n_feat = lax.axis_size("feat")
    feat_index = lax.axis_index("feat")
    seq_index = lax.axis_index("seq")
    own_heads = H // n_feat
    head_dim = width // H
    flat_rows = hidden_in.reshape(prompts * span, width)
    positions = seq_index * span + jnp.arange(span, dtype=jnp.int32)
    live_mask = (positions[None, :] < lengths[:, None]).astype(jnp.float32)
    key_mask = live_mask[:, :, None, None]
    values_own = jnp.dot(flat_rows, w_value, preferred_element_type=jnp.float32).astype(
        jnp.bfloat16
    )
    value_own = values_own.reshape(prompts, span, own_heads, head_dim).astype(jnp.float32)
    query_cols = lax.dynamic_slice_in_dim(w_query, feat_index * own_heads * FD, own_heads * FD, 1)
    key_cols = lax.dynamic_slice_in_dim(w_key, feat_index * own_heads * FD, own_heads * FD, 1)
    query_own = project(flat_rows, query_cols, prompts, span, own_heads, FD)
    key_own = project(flat_rows, key_cols, prompts, span, own_heads, FD)
    key_quad = quad_features(key_own, key_own) * key_mask
    query_quad = quad_features(query_own, query_own)
    span_quad = jnp.einsum("pchf,pchd->phfd", key_quad, value_own, precision=highest)
    norm_span = jnp.sum(key_quad, axis=1)
    key_low = low_features(key_own) * key_mask
    query_low = low_features(query_own)
    span_low = jnp.einsum("pchf,pchd->phfd", key_low, value_own, precision=highest)
    low_norm = jnp.sum(key_low, axis=1)
    empty_states = (
        jnp.zeros_like(span_quad),
        jnp.zeros_like(norm_span),
        jnp.zeros_like(span_low),
        jnp.zeros_like(low_norm),
    )
    pre_quad, pre_norm, pre_low, pre_lnorm = prefix(
        (span_quad, norm_span, span_low, low_norm), "seq", add_states, empty_states
    )
    final_quad, final_norm, final_low, final_lnorm = lax.psum(
        (span_quad, norm_span, span_low, low_norm), "seq"
    )
    num_low = jnp.einsum("pchf,phfd->pchd", query_low, pre_low, precision=highest)
    den_low = jnp.einsum("pchf,phf->pch", query_low, pre_lnorm, precision=highest)
    num_quad = jnp.einsum("pchf,phfd->pchd", query_quad, pre_quad, precision=highest)
    den_quad = jnp.einsum("pchf,phf->pch", query_quad, pre_norm, precision=highest)
    final_quad, final_norm = (
        lax.all_to_all(final_quad, "feat", split_axis=2, concat_axis=1, tiled=True),
        lax.all_to_all(final_norm, "feat", split_axis=2, concat_axis=1, tiled=True),
    )
    scores = jnp.einsum("pthf,puhf->phtu", query_own, key_own, precision=highest)
    kernel = 1.0 + scores * FD ** (-0.5) + scores * scores * (0.5 / FD)
    causal = (jnp.arange(span)[:, None] >= jnp.arange(span)[None, :]).astype(jnp.float32)
    weight = kernel * causal[None, None, :, :] * live_mask[:, None, None, :]
    num_self = jnp.einsum("phtu,puhd->pthd", weight, value_own, precision=highest)
    den_self = jnp.transpose(jnp.sum(weight, axis=3), (0, 2, 1))
    numerator = num_low + num_quad + num_self
    denominator = den_low + den_quad + den_self
    attended = numerator / denominator[..., None] * live_mask[:, :, None, None]
    squares = jnp.sum(attended * attended, axis=(2, 3))
    sum_squares = lax.psum(squares, "feat")
    scaled = attended * lax.rsqrt(sum_squares / width + NORM_FLOOR)[:, :, None, None]
    mixed = scaled.astype(jnp.bfloat16).reshape(prompts, span, own_heads * head_dim)
    owned = (owners == seq_index).astype(jnp.float32)
    state_quad = (owned[:, None, None, None] * final_quad)[None]
    state_low = (owned[:, None, None, None] * final_low)[None]
    norm_quad = (owned[:, None, None] * final_norm)[None]
    norm_low = (owned[:, None, None] * final_lnorm)[None]
    return (mixed, state_quad, state_low, norm_quad, norm_low)


def solution(mesh):
    placed = (P(None, "seq", None), P(), P(), P(None, "feat"), P(), P())
    return jax.shard_map(
        body,
        mesh=mesh,
        in_specs=placed,
        out_specs=(
            P(None, "seq", "feat"),
            P("seq", None, None, "feat", None),
            P("seq", None, "feat", None, None),
            P("seq", None, None, "feat"),
            P("seq", None, "feat", None),
        ),
        check_vma=False,
    )
```

profile of v0, /device:TPU:0, one launch (start us, length us, event | category | flops | bytes accessed | tf_op | source)
XLA Modules:
  0.0 468.9 jit_solution(4810927062687896524)
XLA Ops:
  7.2 4.2 fusion.9
  11.7 0.7 multiply_reduce_fusion
  12.4 2.8 bitcast_multiply_fusion
  15.2 0.9 copy-done.2
  16.1 3.3 convolution_convert_fusion
  19.3 1.3 reshape.151
  20.7 0.6 copy.62
  21.3 5.5 %fusion.36 = f32[4,4,256,128]{3,2,1,0:T(8,128)} fusion(f32[4,256,4,256]{1,3,2,0:T(8,128)} %bitcast_multiply_fusion, bf16[4,256,4,128]{1,3,2,0:T(8,128)(2,1)S(1)} %copy.62), kind=kOutput, calls=%fused_computation.68 | convolution fusion | flops 1610612736 | bytes 7340032 | tf_op jit(solution)/shard_map/pchf,pchd->phfd/dot_general | solution.py:71
  26.8 0.5 copy.66
  27.4 0.1 fusion.17
  27.5 57.1 %all-reduce.2 = (f32[4,4,256]{1,0,2:T(4,128)S(1)}, f32[4,4,17]{2,1,0:T(4,128)S(1)}) all-reduce(f32[4,4,256]{1,0,2:T(4,128)S(1)} %bitcast.91, f32[4,4,17]{2,1,0:T(4,128)S(1)} %fusion.17), channel_id=1, replica_groups=mesh['seq'=8,'feat'=4] {'seq'}, use_global_device_ids=true, to_apply=%region_9.10 | all-reduce | flops 4368 | bytes 34944 | tf_op jit(solution)/shard_map/psum | solution.py:86
  84.7 1.2 reshape.161
  85.8 3.3 all-to-all-start.1
  89.1 0.2 all-gather.8.cloned.1.call-start
  89.3 0.9 fusion.18
  90.2 0.7 copy.55
  91.0 0.1 all_gather.26
  91.1 4.1 fusion.10
  95.4 0.7 multiply_bitcast_fusion.1
  96.1 2.6 multiply_multiply_fusion.1
  98.7 1.5 fusion.1
  100.2 3.9 fusion.2
  104.1 32.0 %all_gather.27 = f32[8,4,4,256]{3,2,1,0:T(4,128)S(1)} all-gather(f32[1,4,4,256]{3,2,1,0:T(4,128)S(1)} %all_gather.26), channel_id=1, replica_groups=mesh['seq'=8,'feat'=4] {'seq'}, dimensions={0}, use_global_device_ids=true | all-gather | bytes 147456 | tf_op jit(solution)/shard_map/all_gather | solution.py:13
  136.1 33.0 %all-gather.2 = f32[32,4,17]{2,1,0:T(4,128)S(1)} all-gather(f32[4,4,17]{2,1,0:T(4,128)S(1)} %fusion.17), channel_id=4, replica_groups=mesh['seq'=8,'feat'=4] {'seq'}, dimensions={0}, use_global_device_ids=true | all-gather | bytes 9792 | tf_op jit(solution)/shard_map/all_gather | solution.py:13
  169.1 0.5 broadcast.92
  169.6 0.7 reduce.1
  170.3 0.7 reshape.162
  171.0 0.2 copy.68
  171.2 0.7 broadcast_multiply_fusion.4
  171.9 94.8 %all-gather.6.cloned.1.call-done = f32[32,4,256,128]{3,2,1,0:T(8,128)} async-done(((f32[4,4,256,128]{3,2,1,0:T(8,128)}), f32[32,4,256,128]{3,2,1,0:T(8,128)}) %all-gather.6.cloned.1.call-update) | async-done | bytes 16777232 | tf_op jit(solution)/shard_map/all_gather | solution.py:13
  266.7 0.7 all-reduce.6.cloned.1.call-update
  267.4 41.0 %all-gather.8.cloned.1.call-done = f32[32,4,17,128]{3,1,2,0:T(4,128)} async-done(((f32[4,4,17,128]{3,1,2,0:T(4,128)}), f32[32,4,17,128]{3,1,2,0:T(4,128)}) %all-gather.8.cloned.1.call-update) | async-done | bytes 1114128 | tf_op jit(solution)/shard_map/all_gather | solution.py:13
  308.4 0.2 broadcast_in_dim.12
  308.7 0.2 while.16
  308.9 0.4 fusion.13
  309.3 3.2 fusion.15
  312.4 4.3 fusion.26
  316.7 101.8 %all-reduce.6.cloned.1.call-done = (f32[4,4,256,128]{3,2,1,0:T(8,128)}, f32[4,4,17,128]{3,2,1,0:T(8,128)}) async-done(((f32[4,4,256,128]{3,2,1,0:T(8,128)}, f32[4,4,17,128]{3,2,1,0:T(8,128)}), (f32[4,4,256,128]{3,2,1,0:T(8,128)}, f32[4,4,17,128]{3,2,1,0:T(8,128)})) %all-reduce.6.cloned.1.call-update) | async-done | bytes 2236432 | tf_op jit(solution)/shard_map/psum | solution.py:86
  418.5 4.3 copy.64
  422.8 4.4 all-to-all-start
  427.3 8.3 %multiply_reduce_fusion.1 = (f32[4,256]{1,0:T(4,128)S(1)}, f32[4,256,4,128]{1,3,2,0:T(8,128)}) fusion(f32[4,256]{1,0:T(4,128)S(1)} %compare_convert_fusion, f32[4,256,4]{1,2,0:T(4,128)S(1)} %fusion.25, f32[4,4,128,256]{3,2,1,0:T(8,128)} %fusion.2, f32[4,4,128,256]{3,2,1,0:T(8,128)} %fusion.15, f32[4,4,256,128]{3,2,1,0:T(8,128)S(1)} %get-tuple-element.62, ...), kind=kOutput, calls=%fused_computation.15 | convolution fusion | flops 1613757440 | bytes 12607488 | tf_op jit(solution)/shard_map/pchf,phfd->pchd/dot_general | solution.py:91
  435.6 18.8 %psum.35 = f32[4,256]{1,0:T(4,128)S(1)} all-reduce(f32[4,256]{1,0:T(4,128)S(1)} %get-tuple-element.123), channel_id=1, replica_groups=mesh['seq'=8,'feat'=4] {'feat'}, use_global_device_ids=true, to_apply=%region_6.7 | all-reduce | flops 1024 | bytes 8192 | tf_op jit(solution)/shard_map/psum | solution.py:107
  454.4 1.8 multiply_convert_fusion
  456.3 1.3 copy.69
  457.6 0.1 multiply_bitcast_fusion
  457.7 0.7 copy.70
  458.4 2.4 copy.65
  460.8 1.6 broadcast_multiply_fusion.1
  (35 shorter events, 0.6 us)
Async XLA Ops:
  7.2 8.0 %copy-start = (bf16[2048,512]{1,0:T(8,128)(2,1)S(1)}, bf16[2048,512]{1,0:T(8,128)(2,1)}, u32[]{:S(2)}) copy-start(bf16[2048,512]{1,0:T(8,128)(2,1)} %param.11) | copy-start | bytes 6291460
  7.2 4.4 copy-start.5
  7.2 259.5 %all-gather.6.cloned.1.call-start = ((), (), s32[]{:S(2)}) async-start(), calls=%async_computation.2 | async-start | bytes 18874368 | tf_op jit(solution)/shard_map/all_gather | solution.py:13
  12.4 3.7 copy-start.2
  84.6 10.7 %copy-start.6 = (s32[4]{0:T(128)S(1)}, s32[4]{0:T(128)}, u32[]{:S(2)}) copy-start(s32[4]{0:T(128)} %param.13) | copy-start | bytes 52
  85.8 83.2 %all-to-all-start.1 = ((f32[4,1,1024]{2,1,0:T(1,128)}), f32[4,1,1024]{2,1,0:T(1,128)S(1)}, u32[]{:S(2)}, u32[]{:S(2)}) async-start(f32[4,1,1024]{2,1,0:T(1,128)} %reshape.161), calls=%async_computation.1 | async-start | bytes 32768 | tf_op jit(solution)/shard_map/all_to_all | solution.py:95
  89.1 219.3 %all-gather.8.cloned.1.call-start = ((), (), s32[]{:S(2)}) async-start(), calls=%async_computation.3 | async-start | bytes 1253376 | tf_op jit(solution)/shard_map/all_gather | solution.py:13
  90.2 8.4 %copy-start.3 = (f32[4,4,17,128]{3,2,1,0:T(8,128)}, f32[4,4,17,128]{3,2,1,0:T(8,128)S(1)}, u32[]{:S(2)}) copy-start(f32[4,4,17,128]{3,2,1,0:T(8,128)S(1)} %fusion.18) | copy-start | bytes 417796
  266.6 151.9 %all-reduce.6.cloned.1.call-start = ((), (), s32[]{:S(2)}) async-start(), calls=%async_computation.4 | async-start | bytes 4587520 | tf_op jit(solution)/shard_map/psum | solution.py:86
  422.8 35.6 %all-to-all-start = ((f32[4,4,256,128]{3,1,0,2:T(4,128)}), f32[4,4,256,128]{3,1,0,2:T(4,128)}, u32[]{:S(2)}, u32[]{:S(2)}) async-start(f32[4,4,256,128]{3,1,0,2:T(4,128)} %copy.64), calls=%async_computation | async-start | bytes 4194304 | tf_op jit(solution)/shard_map/all_to_all | solution.py:94
  435.6 22.0 %copy-start.4 = (f32[4,4,17,128]{3,2,1,0:T(8,128)S(1)}, f32[4,4,17,128]{3,2,1,0:T(8,128)}, u32[]{:S(2)}) copy-start(f32[4,4,17,128]{3,2,1,0:T(8,128)} %get-tuple-element.118) | copy-start | bytes 417796
  458.4 4.0 copy-start.1
Sparse Core Ops, SparseCore 0:
  26.9 239.6 all-gather.5
  269.4 38.9 all-gather.7
  312.7 105.7 all-reduce.5
where the time goes:
time: 470 us; the launch traced here: 469 us
  waiting for transfers between devices  238 us (51%)
  blocking collectives  141 us (30%)
  matrix products  39.6 us (8%)
  local copies, waits for them, and re-layouts  15.8 us (3%)
  between operations  14 us (3%)
  other arithmetic  12 us (3%)
  starting transfers between devices  7.96 us (2%)
    all_gather x2, waiting for transfers between devices, prefix(): gathered = jax.tree.map(lambda a: lax.all_gather(a, axis), part)  136 us
    psum x1, waiting for transfers between devices, body(): lax.psum((span_quad, norm_span, span_low, low_norm), 'seq')  102 us
    all_gather x2, blocking collectives, prefix(): gathered = jax.tree.map(lambda a: lax.all_gather(a, axis), part)  65 us
    psum x1, blocking collectives, body(): lax.psum((span_quad, norm_span, span_low, low_norm), 'seq')  57.1 us
    psum x1, blocking collectives, body(): sum_squares = lax.psum(squares, 'feat')  18.8 us
  transfers between devices with their start and end apart: 5, of which 3 were waited for; matrix products, arithmetic and copies ran while one was open for 8% of the time, Pallas kernels for 0%

commit v1 on v0

--- a/solution.py
+++ b/solution.py
@@ -104,7 +104,7 @@
     denominator = den_low + den_quad + den_self
     attended = numerator / denominator[..., None] * live_mask[:, :, None, None]
     squares = jnp.sum(attended * attended, axis=(2, 3))
-    sum_squares = lax.psum(squares, "feat")
+    sum_squares = jnp.sum(lax.all_gather(squares, "feat"), axis=0)
     scaled = attended * lax.rsqrt(sum_squares / width + NORM_FLOOR)[:, :, None, None]
     mixed = scaled.astype(jnp.bfloat16).reshape(prompts, span, own_heads * head_dim)
     owned = (owners == seq_index).astype(jnp.float32)

time: 470 us -> 469 us (level)
    psum x1 -> x0, blocking collectives: 18.8 us -> none  [body(): sum_squares = lax.psum(squares, 'feat')]
    all_gather x0 -> x1, blocking collectives: none -> 18.3 us  [body(): sum_squares = jnp.sum(lax.all_gather(squares, 'feat'), axis=0)]
where the time goes in v1:
time: 469 us; the launch traced here: 468 us
  waiting for transfers between devices  238 us (51%)
  blocking collectives  140 us (30%)
  matrix products  39.6 us (8%)
  local copies, waits for them, and re-layouts  15.8 us (3%)
  between operations  14 us (3%)
  other arithmetic  12 us (3%)
  starting transfers between devices  7.96 us (2%)
    all_gather x2, waiting for transfers between devices, prefix(): gathered = jax.tree.map(lambda a: lax.all_gather(a, axis), part)  136 us
    psum x1, waiting for transfers between devices, body(): lax.psum((span_quad, norm_span, span_low, low_norm), 'seq')  102 us
    all_gather x2, blocking collectives, prefix(): gathered = jax.tree.map(lambda a: lax.all_gather(a, axis), part)  65 us
    psum x1, blocking collectives, body(): lax.psum((span_quad, norm_span, span_low, low_norm), 'seq')  57.1 us
    all_gather x1, blocking collectives, body(): sum_squares = jnp.sum(lax.all_gather(squares, 'feat'), axis=0)  18.3 us
  transfers between devices with their start and end apart: 5, of which 3 were waited for; matrix products, arithmetic and copies ran while one was open for 8% of the time, Pallas kernels for 0%

profile of v1, /device:TPU:0, one launch (start us, length us, event | category | flops | bytes accessed | tf_op | source)
XLA Modules:
  0.0 468.4 jit_solution(9084697610891866758)
XLA Ops:
  7.2 4.2 fusion.9
  11.7 0.7 multiply_reduce_fusion
  12.4 2.8 bitcast_multiply_fusion
  15.2 0.9 copy-done.2
  16.1 3.3 convolution_convert_fusion
  19.3 1.3 reshape.155
  20.7 0.6 copy.62
  21.3 5.5 %fusion.36 = f32[4,4,256,128]{3,2,1,0:T(8,128)} fusion(f32[4,256,4,256]{1,3,2,0:T(8,128)} %bitcast_multiply_fusion, bf16[4,256,4,128]{1,3,2,0:T(8,128)(2,1)S(1)} %copy.62), kind=kOutput, calls=%fused_computation.68 | convolution fusion | flops 1610612736 | bytes 7340032 | tf_op jit(solution)/shard_map/pchf,pchd->phfd/dot_general | solution.py:71
  26.8 0.5 copy.66
  27.4 0.1 fusion.17
  27.5 57.1 %all-reduce.2 = (f32[4,4,256]{1,0,2:T(4,128)S(1)}, f32[4,4,17]{2,1,0:T(4,128)S(1)}) all-reduce(f32[4,4,256]{1,0,2:T(4,128)S(1)} %bitcast.92, f32[4,4,17]{2,1,0:T(4,128)S(1)} %fusion.17), channel_id=1, replica_groups=mesh['seq'=8,'feat'=4] {'seq'}, use_global_device_ids=true, to_apply=%region_9.10 | all-reduce | flops 4368 | bytes 34944 | tf_op jit(solution)/shard_map/psum | solution.py:86
  84.7 1.2 reshape.169
  85.8 3.3 all-to-all-start.1
  89.1 0.2 all-gather.10.cloned.1.call-start
  89.3 0.9 fusion.18
  90.2 0.7 copy.55
  91.0 0.1 all_gather.32
  91.1 4.1 fusion.10
  95.4 0.7 multiply_bitcast_fusion.1
  96.1 2.6 multiply_multiply_fusion.1
  98.7 1.5 fusion.1
  100.2 3.9 fusion.2
  104.1 32.0 %all_gather.33 = f32[8,4,4,256]{3,2,1,0:T(4,128)S(1)} all-gather(f32[1,4,4,256]{3,2,1,0:T(4,128)S(1)} %all_gather.32), channel_id=1, replica_groups=mesh['seq'=8,'feat'=4] {'seq'}, dimensions={0}, use_global_device_ids=true | all-gather | bytes 147456 | tf_op jit(solution)/shard_map/all_gather | solution.py:13
  136.1 33.0 %all-gather.2 = f32[32,4,17]{2,1,0:T(4,128)S(1)} all-gather(f32[4,4,17]{2,1,0:T(4,128)S(1)} %fusion.17), channel_id=4, replica_groups=mesh['seq'=8,'feat'=4] {'seq'}, dimensions={0}, use_global_device_ids=true | all-gather | bytes 9792 | tf_op jit(solution)/shard_map/all_gather | solution.py:13
  169.1 0.5 broadcast.99
  169.6 0.7 reduce.2
  170.3 0.7 reshape.170
  171.0 0.2 copy.68
  171.2 0.7 broadcast_multiply_fusion.4
  171.9 94.8 %all-gather.8.cloned.1.call-done = f32[32,4,256,128]{3,2,1,0:T(8,128)} async-done(((f32[4,4,256,128]{3,2,1,0:T(8,128)}), f32[32,4,256,128]{3,2,1,0:T(8,128)}) %all-gather.8.cloned.1.call-update) | async-done | bytes 16777232 | tf_op jit(solution)/shard_map/all_gather | solution.py:13
  266.7 0.7 all-reduce.6.cloned.1.call-update
  267.4 41.0 %all-gather.10.cloned.1.call-done = f32[32,4,17,128]{3,1,2,0:T(4,128)} async-done(((f32[4,4,17,128]{3,1,2,0:T(4,128)}), f32[32,4,17,128]{3,1,2,0:T(4,128)}) %all-gather.10.cloned.1.call-update) | async-done | bytes 1114128 | tf_op jit(solution)/shard_map/all_gather | solution.py:13
  308.4 0.2 broadcast_in_dim.12
  308.7 0.2 while.16
  308.9 0.4 fusion.13
  309.3 3.2 fusion.15
  312.4 4.3 fusion.26
  316.7 101.8 %all-reduce.6.cloned.1.call-done = (f32[4,4,256,128]{3,2,1,0:T(8,128)}, f32[4,4,17,128]{3,2,1,0:T(8,128)}) async-done(((f32[4,4,256,128]{3,2,1,0:T(8,128)}, f32[4,4,17,128]{3,2,1,0:T(8,128)}), (f32[4,4,256,128]{3,2,1,0:T(8,128)}, f32[4,4,17,128]{3,2,1,0:T(8,128)})) %all-reduce.6.cloned.1.call-update) | async-done | bytes 2236432 | tf_op jit(solution)/shard_map/psum | solution.py:86
  418.5 4.3 copy.64
  422.8 4.4 all-to-all-start
  427.3 8.3 %multiply_reduce_fusion.1 = (f32[4,256]{1,0:T(4,128)S(1)}, f32[4,256,4,128]{1,3,2,0:T(8,128)}) fusion(f32[4,256]{1,0:T(4,128)S(1)} %compare_convert_fusion, f32[4,256,4]{1,2,0:T(4,128)S(1)} %fusion.25, f32[4,4,128,256]{3,2,1,0:T(8,128)} %fusion.2, f32[4,4,128,256]{3,2,1,0:T(8,128)} %fusion.15, f32[4,4,256,128]{3,2,1,0:T(8,128)S(1)} %get-tuple-element.62, ...), kind=kOutput, calls=%fused_computation.15 | convolution fusion | flops 1613757440 | bytes 12607488 | tf_op jit(solution)/shard_map/pchf,phfd->pchd/dot_general | solution.py:91
  435.6 18.3 %all-gather.4 = f32[4,4,256]{2,1,0:T(4,128)S(1)} all-gather(f32[1,4,256]{2,1,0:T(4,128)S(1)} %bitcast.100), channel_id=5, replica_groups=mesh['seq'=8,'feat'=4] {'feat'}, dimensions={0}, use_global_device_ids=true | all-gather | bytes 20480 | tf_op jit(solution)/shard_map/all_gather | solution.py:107
  453.9 1.8 multiply_convert_fusion
  455.7 1.3 copy.69
  457.1 0.1 multiply_bitcast_fusion
  457.1 0.7 copy.70
  457.8 2.4 copy.65
  460.3 1.6 broadcast_multiply_fusion.1
  (36 shorter events, 0.6 us)
Async XLA Ops:
  7.2 8.0 %copy-start = (bf16[2048,512]{1,0:T(8,128)(2,1)S(1)}, bf16[2048,512]{1,0:T(8,128)(2,1)}, u32[]{:S(2)}) copy-start(bf16[2048,512]{1,0:T(8,128)(2,1)} %param.11) | copy-start | bytes 6291460
  7.2 4.4 copy-start.5
  7.2 259.5 %all-gather.8.cloned.1.call-start = ((), (), s32[]{:S(2)}) async-start(), calls=%async_computation.2 | async-start | bytes 18874368 | tf_op jit(solution)/shard_map/all_gather | solution.py:13
  12.4 3.7 copy-start.2
  84.6 10.7 %copy-start.6 = (s32[4]{0:T(128)S(1)}, s32[4]{0:T(128)}, u32[]{:S(2)}) copy-start(s32[4]{0:T(128)} %param.13) | copy-start | bytes 52
  85.8 83.2 %all-to-all-start.1 = ((f32[4,1,1024]{2,1,0:T(1,128)}), f32[4,1,1024]{2,1,0:T(1,128)S(1)}, u32[]{:S(2)}, u32[]{:S(2)}) async-start(f32[4,1,1024]{2,1,0:T(1,128)} %reshape.169), calls=%async_computation.1 | async-start | bytes 32768 | tf_op jit(solution)/shard_map/all_to_all | solution.py:95
  89.1 219.3 %all-gather.10.cloned.1.call-start = ((), (), s32[]{:S(2)}) async-start(), calls=%async_computation.3 | async-start | bytes 1253376 | tf_op jit(solution)/shard_map/all_gather | solution.py:13
  90.2 8.4 %copy-start.3 = (f32[4,4,17,128]{3,2,1,0:T(8,128)}, f32[4,4,17,128]{3,2,1,0:T(8,128)S(1)}, u32[]{:S(2)}) copy-start(f32[4,4,17,128]{3,2,1,0:T(8,128)S(1)} %fusion.18) | copy-start | bytes 417796
  266.6 151.9 %all-reduce.6.cloned.1.call-start = ((), (), s32[]{:S(2)}) async-start(), calls=%async_computation.4 | async-start | bytes 4587520 | tf_op jit(solution)/shard_map/psum | solution.py:86
  422.8 35.1 %all-to-all-start = ((f32[4,4,256,128]{3,1,0,2:T(4,128)}), f32[4,4,256,128]{3,1,0,2:T(4,128)}, u32[]{:S(2)}, u32[]{:S(2)}) async-start(f32[4,4,256,128]{3,1,0,2:T(4,128)} %copy.64), calls=%async_computation | async-start | bytes 4194304 | tf_op jit(solution)/shard_map/all_to_all | solution.py:94
  435.6 21.4 %copy-start.4 = (f32[4,4,17,128]{3,2,1,0:T(8,128)S(1)}, f32[4,4,17,128]{3,2,1,0:T(8,128)}, u32[]{:S(2)}) copy-start(f32[4,4,17,128]{3,2,1,0:T(8,128)} %get-tuple-element.118) | copy-start | bytes 417796
  457.8 4.0 copy-start.1
Sparse Core Ops, SparseCore 0:
  26.9 239.6 all-gather.7
  269.4 38.9 all-gather.9
  312.7 105.7 all-reduce.5
